TPU v7x, 32 devices: a whole 2x2x4 slice. The times are simulated.
32 devices in a mesh: expert: 4 (over x, core), row: 2 (over y), col: 4 (over z).
Axes of the slice: x: 2, y: 2, z: 4, core: 2. Of those that a mesh axis runs over, the one named last changes fastest.
Arguments:
- weights: bfloat16 [4, 4096, 7168], P('expert', 'row', 'col'), may hold values from -210 to 210
- inputs: bfloat16 [4, 1024, 4096], P('expert', ('row', 'col')), may hold values from -80 to 80
- cotangents: bfloat16 [4, 1024, 7168], P('expert', ('row', 'col')), may hold values from -150 to 150
- row_state: float32 [4, 4096], P('expert', 'row'), may hold values from 0.00089 to 0.91
- col_state: float32 [4, 7168], P('expert', 'col'), may hold values from 0.00089 to 0.91
Outputs:
- scaled_update: float32 [4, 4096, 7168], P('expert', 'row', 'col')
- new_row_state: float32 [4, 4096], P('expert', 'row')
- new_col_state: float32 [4, 7168], P('expert', 'col')
All inputs are finite; a program needn't handle non-finite values.
Results may differ from a plain program's by a relative error of at most 0.0003.
Values may be sent and summed in bfloat16 or wider, within the bound.
A program may use at most 128 MiB of HBM per device.

v0:
```python
import jax
import jax.numpy as jnp
from jax import lax
from jax.sharding import PartitionSpec as P

STEP = 10


eps_square = 1e-30


def reduce_factors(row_part, col_part):
    row_total = lax.psum(row_part, "col")
    col_total = lax.psum(col_part, "row")
    return (row_total, col_total)


def body(weights, inputs, cotangents, row_state, col_state):
    matrices, rows_here, cols_here = weights.shape
    model_width = inputs.shape[2]
    hidden_width = cotangents.shape[2]
    row_count = lax.axis_size("row")
    col_count = lax.axis_size("col")
    block_rows = inputs.shape[1]
    inputs_split = lax.all_to_all(inputs, "row", split_axis=2, concat_axis=1, tiled=True)
    hidden_split = lax.all_to_all(cotangents, "col", split_axis=2, concat_axis=1, tiled=True)
    hidden_all = lax.all_gather(hidden_split, "row", axis=1, tiled=True)
    hidden_blocks = hidden_all.reshape(matrices, row_count, col_count, block_rows, cols_here)
    shard_rows = lax.all_gather(inputs_split, "col", axis=1, tiled=True)
    block_count = shard_rows.shape[1] // (row_count * block_rows)
    input_blocks = shard_rows.reshape(matrices, block_count, row_count, block_rows, rows_here)
    gradient = jnp.einsum(
        "mkrti,mrktj->mij", input_blocks, hidden_blocks, preferred_element_type=jnp.float32
    )
    decay_rate = 1.0 - STEP ** (-0.8)
    entry_count = model_width * hidden_width
    squares = gradient * gradient
    weights_wide = weights.astype(jnp.float32)
    weight_squares = jnp.sum(weights_wide * weights_wide, axis=(1, 2))
    squared_total = lax.psum(jnp.sum(squares), ("expert", "row", "col"))
    clip_scale = 1.0 / jnp.maximum(
        1.0, jnp.sqrt(squared_total / (matrices * lax.axis_size("expert") * entry_count))
    )
    clipped = clip_scale * gradient
    clipped_squares = clipped * clipped + eps_square
    row_sum, col_sum = reduce_factors(
        jnp.sum(clipped_squares, axis=2), jnp.sum(clipped_squares, axis=1)
    )
    new_rows = decay_rate * row_state + (1.0 - decay_rate) * (row_sum / hidden_width)
    new_cols = decay_rate * col_state + (1.0 - decay_rate) * (col_sum / model_width)
    row_average = lax.psum(jnp.sum(new_rows, axis=1), "row") / model_width
    second = new_rows[:, :, None] * new_cols[:, None, :] / row_average[:, None, None]
    update = clipped / jnp.sqrt(second)
    update_squares = jnp.sum(update * update, axis=(1, 2))
    update_total, weight_total = lax.psum((update_squares, weight_squares), ("row", "col"))
    update = update / jnp.maximum(1.0, jnp.sqrt(update_total / entry_count))[:, None, None]
    weight_rms = jnp.sqrt(weight_total / entry_count)
    return (weight_rms[:, None, None] * update, new_rows, new_cols)


def solution(mesh):
    in_specs = (
        P("expert", "row", "col"),
        P("expert", ("row", "col"), None),
        P("expert", ("row", "col"), None),
        P("expert", "row"),
        P("expert", "col"),
    )
    out_specs = (P("expert", "row", "col"), P("expert", "row"), P("expert", "col"))
    return jax.shard_map(body, mesh=mesh, in_specs=in_specs, out_specs=out_specs, check_vma=False)
```

profile of v0, /device:TPU:0, one launch (start us, length us, event | category | flops | bytes accessed | tf_op | source)
XLA Modules:
  0.0 391.4 jit_solution(717447790940742205)
XLA Ops:
  7.2 0.0 all-gather.5.cloned.1.call-start
  7.2 8.6 %copy.18 = bf16[1,128,7168]{1,0,2:T(2,128)(2,1)} copy(bf16[1,128,7168]{2,1,0:T(8,128)(2,1)} %param.7) | data formatting | bytes 3670016 | tf_op args[2]
  15.8 0.5 broadcast.17
  16.3 41.1 %reduce.13 = bf16[7168,128]{1,0:T(8,128)(2,1)} reduce(bf16[7168,1,128]{2,1,0:T(2,128)(2,1)} %bitcast.44, bf16[]{:T(256)} %broadcast.17), dimensions={1}, to_apply=%bitcast.41.reduce_sub_computation | reduce | bytes 3670018
  57.4 2.5 reshape.55
  59.9 48.8 %all_to_all.36 = bf16[4,2,114688]{2,1,0:T(2,128)(2,1)} all-to-all(bf16[4,2,114688]{2,1,0:T(2,128)(2,1)S(1)} %reshape.55), channel_id=1, replica_groups=mesh['expert'=4,'row'=2,'col'=4] {'col'}, dimensions={0} | all-to-all | bytes 3670016 | tf_op jit(solution)/shard_map/all_to_all | solution.py:26
  108.7 4.7 %reshape.56 = bf16[7168,1,128]{2,1,0:T(2,128)(2,1)} reshape(bf16[4,2,114688]{2,1,0:T(2,128)(2,1)} %all_to_all.36) | data formatting | bytes 3670016
  113.4 2.3 copy.25
  115.7 2.4 copy.19
  118.1 0.0 all-gather.5.cloned.1.call-update
  118.1 0.2 all-gather.3.cloned.1.call-start
  118.4 0.0 copy-done
  118.4 2.8 copy.16
  121.2 22.4 %reduce.12 = bf16[4096,128]{1,0:T(8,128)(2,1)S(1)} reduce(bf16[4096,1,128]{2,1,0:T(2,128)(2,1)S(1)} %bitcast.47, bf16[]{:T(256)} %broadcast.17), dimensions={1}, to_apply=%bitcast.39.reduce_sub_computation | reduce | bytes 2097154
  143.6 0.3 reshape.53
  143.9 28.1 %all_to_all.37 = bf16[2,2,131072]{2,1,0:T(2,128)(2,1)S(1)} all-to-all(bf16[2,2,131072]{2,1,0:T(2,128)(2,1)S(1)} %reshape.53), channel_id=1, replica_groups=mesh['expert'=4,'row'=2,'col'=4] {'row'}, dimensions={0} | all-to-all | bytes 2097152 | tf_op jit(solution)/shard_map/all_to_all | solution.py:25
  172.0 0.9 reshape.54
  173.0 0.1 copy.24
  173.1 1.4 copy.17
  174.5 0.0 all-gather.3.cloned.1.call-update
  174.5 7.5 %multiply_reduce_fusion.1 = f32[]{:T(128)} fusion(bf16[1,2048,1792]{2,1,0:T(8,128)(2,1)} %param.5), kind=kLoop, calls=%fused_computation.7 | loop fusion | flops 11010047 | bytes 7340036 | tf_op jit(solution)/shard_map/reduce_sum | solution.py:39
  182.0 79.9 %all-gather.3.cloned.1.call-done = bf16[1,1024,2048]{2,1,0:T(8,128)(2,1)} async-done(((bf16[1,256,2048]{2,1,0:T(8,128)(2,1)}), bf16[1,1024,2048]{2,1,0:T(8,128)(2,1)}) %all-gather.3.cloned.1.call-update) | async-done | bytes 4194320 | tf_op jit(solution)/shard_map/all_gather | solution.py:29
  261.9 15.2 %fusion = (f32[]{:T(128)}, f32[2048,1792,1,1]{1,0,3,2:T(8,128)}) fusion(bf16[4,2,128,2048]{3,2,1,0:T(8,128)(2,1)} %bitcast.55, bf16[2,4,128,1792]{3,2,1,0:T(8,128)(2,1)} %bitcast.56), kind=kOutput, calls=%fused_computation.2 | convolution fusion | flops 7523532800 | bytes 22544388 | tf_op jit(solution)/shard_map/mkrti,mrktj->mij/dot_general | solution.py:32
  277.1 38.9 %psum.43 = f32[]{:T(128)} all-reduce(f32[]{:T(128)} %get-tuple-element.13), channel_id=1, replica_groups=mesh['expert'=4,'row'=2,'col'=4] {'expert','row','col'}, use_global_device_ids=true, to_apply=%region_3.0 | all-reduce | flops 1 | bytes 8 | tf_op jit(solution)/shard_map/psum | solution.py:40
  316.7 8.1 %fusion.1 = (f32[1792]{0:T(1024)S(1)}, f32[2048]{0:T(1024)S(1)}) fusion(f32[2048,1792,1,1]{1,0,3,2:T(8,128)} %get-tuple-element.14, f32[]{:T(128)S(6)} %div.46), kind=kLoop, calls=%fused_computation.8 | loop fusion | flops 18346240 | bytes 14695428 | tf_op jit(solution)/shard_map/reduce_sum | solution.py:47
  324.8 10.8 %psum.44 = f32[1,2048]{1,0:T(1,128)S(1)} all-reduce(f32[1,2048]{1,0:T(1,128)S(1)} %bitcast.54), channel_id=1, replica_groups=mesh['expert'=4,'row'=2,'col'=4] {'col'}, use_global_device_ids=true, to_apply=%region_5.0 | all-reduce | flops 2048 | bytes 16384 | tf_op jit(solution)/shard_map/psum | solution.py:13
  335.6 0.6 fusion.6
  336.2 6.0 %all-reduce.1 = (f32[1]{0:T(128)}, f32[1,1792]{1,0:T(1,128)S(1)}) all-reduce(f32[1]{0:T(128)} %bitcast.12, f32[1,1792]{1,0:T(1,128)S(1)} %reduce_sum.70), channel_id=1, replica_groups=mesh['expert'=4,'row'=2,'col'=4] {'row'}, use_global_device_ids=true, to_apply=%region_9.0 | all-reduce | flops 1793 | bytes 14344 | tf_op jit(solution)/shard_map/psum | solution.py:51
  342.9 0.6 fusion.5
  343.6 8.9 %multiply_reduce_fusion = f32[]{:T(128)} fusion(f32[]{:T(128)} %bitcast.13, f32[1792]{0:T(1024)S(1)} %get-tuple-element.9, f32[2048]{0:T(1024)S(1)} %bitcast.52, f32[2048,1792,1,1]{1,0,3,2:T(8,128)} %get-tuple-element.14, f32[]{:T(128)S(6)} %div.46), kind=kLoop, calls=%fused_computation.4 | loop fusion | flops 22020096 | bytes 14695436 | tf_op jit(solution)/shard_map/reduce_sum | solution.py:54
  352.4 19.1 %all-reduce = (f32[1]{0:T(128)}, f32[1]{0:T(128)}) all-reduce(f32[1]{0:T(128)} %bitcast.14, f32[1]{0:T(128)} %bitcast), channel_id=1, replica_groups=mesh['expert'=4,'row'=2,'col'=4] {'row','col'}, use_global_device_ids=true, to_apply=%region_11.0 | all-reduce | flops 2 | bytes 16 | tf_op jit(solution)/shard_map/psum | solution.py:55
  372.8 11.8 %multiply_bitcast_fusion = f32[1,2048,1792]{2,1,0:T(8,128)} fusion(f32[]{:T(128)} %bitcast.15, f32[]{:T(128)} %bitcast.1, f32[]{:T(128)} %bitcast.13, f32[1792]{0:T(1024)S(1)} %get-tuple-element.9, f32[2048]{0:T(1024)S(1)} %bitcast.53, f32[2048,1792,1,1]{1,0,3,2:T(8,128)} %get-tuple-element.14, f32[]{:T(128)S(6)} %div.46), kind=kLoop, calls=%fused_computation.3 | loop fusion | flops 22020096 | bytes 29375504 | tf_op jit(solution)/shard_map/mul | solution.py:58
  (9 shorter events, 0.0 us)
Async XLA Ops:
  7.2 174.8 %all-gather.5.cloned.1.call-start = ((), (), s32[]{:S(2)}) async-start(), calls=%async_computation.3 | async-start | bytes 5505024 | tf_op jit(solution)/shard_map/all_gather | solution.py:27
  16.3 102.1 %copy-start = (bf16[1,128,4096]{2,1,0:T(8,128)(2,1)S(1)}, bf16[1,128,4096]{2,1,0:T(8,128)(2,1)}, u32[]{:S(2)}) copy-start(bf16[1,128,4096]{2,1,0:T(8,128)(2,1)} %param.6) | copy-start | bytes 3145732
  118.1 143.7 %all-gather.3.cloned.1.call-start = ((), (), s32[]{:S(2)}) async-start(), calls=%async_computation.2 | async-start | bytes 5242880 | tf_op jit(solution)/shard_map/all_gather | solution.py:29
  277.1 58.5 %copy-start.2 = (f32[1,2048]{1,0:T(1,128)S(1)}, f32[1,2048]{1,0:T(1,128)}, u32[]{:S(2)}) copy-start(f32[1,2048]{1,0:T(1,128)} %param.8) | copy-start | bytes 24580
  277.1 65.8 %copy-start.3 = (f32[1,1792]{1,0:T(1,128)S(1)}, f32[1,1792]{1,0:T(1,128)}, u32[]{:S(2)}) copy-start(f32[1,1792]{1,0:T(1,128)} %param.9) | copy-start | bytes 21508
  336.2 48.4 %copy-start.1 = (f32[1,2048]{1,0:T(1,128)}, f32[1,2048]{1,0:T(1,128)S(1)}, u32[]{:S(2)}) copy-start(f32[1,2048]{1,0:T(1,128)S(1)} %get-tuple-element.12) | copy-start | bytes 24580
Sparse Core Ops, SparseCore 0:
  118.3 61.2 all-gather.4
  181.1 80.7 all-gather.2
where the time goes:
time: 392 us; the launch traced here: 391 us
  blocking collectives  152 us (39%)
  other arithmetic  101 us (26%)
  waiting for transfers between devices  79.9 us (20%)
  local copies, waits for them, and re-layouts  26.6 us (7%)
  between operations  16.8 us (4%)
  matrix products  15.2 us (4%)
    all_gather x1, waiting for transfers between devices, body(): shard_rows = lax.all_gather(inputs_split, 'col', axis=1, tiled=True)  79.9 us
    unnamed x2, other arithmetic  63.5 us
    all_to_all x1, blocking collectives, body(): lax.all_to_all(cotangents, 'col', split_axis=2, concat_axis=1, tiled=True)  48.8 us
    psum x1, blocking collectives, body(): squared_total = lax.psum(jnp.sum(squares), ('expert', 'row', 'col'))  38.9 us
    all_to_all x1, blocking collectives, body(): lax.all_to_all(inputs, 'row', split_axis=2, concat_axis=1, tiled=True)  28.1 us
    unnamed x17, local copies, waits for them, and re-layouts  22.7 us
    psum x1, blocking collectives, body(): lax.psum((update_squares, weight_squares), ('row', 'col'))  19.1 us
    dot_general x1, matrix products, body(): jnp.einsum('mkrti,mrktj->mij', input_blocks, hidden_blocks, preferred_ele...  15.2 us
  transfers between devices with their start and end apart: 2, of which 1 were waited for; matrix products, arithmetic and copies ran while one was open for 9% of the time, Pallas kernels for 0%

commit v1 on v0

v1 whole, which is shorter than its diff:
```python
import functools

import jax
import jax.numpy as jnp
from jax import lax
from jax.experimental import pallas as pl
from jax.experimental.pallas import tpu as pltpu
from jax.sharding import PartitionSpec as P

STEP = 10
TILE = 256
CHUNKS = 4

eps_square = 1e-30


def kernel(
    E, Y, Z, total_entries, model_width, hidden_width,
    w_hbm, x_hbm, c_hbm, row_state, col_state,
    g_hbm, new_rows, new_cols, row_factor, col_factor,
    wbuf, xbuf, cbuf, grad, row_part, col_part, col_recv, row_recv, sq_recv, fin_recv,
    sx, rx, sxy, sc, rc, scy, local, out_sem,
    row_send_sem, row_recv_sem, col_send_sem, col_recv_sem, sq_send_sem, sq_recv_sem, fin_send_sem, fin_recv_sem,
):
    e, y, z = lax.axis_index("expert"), lax.axis_index("row"), lax.axis_index("col")
    other = 1 - y
    tokens = x_hbm.shape[0]
    rows, cols = grad.shape
    tiles = rows // TILE
    piece = tokens // CHUNKS
    decay_rate = 1.0 - STEP ** (-0.8)

    def dev(e_, y_, z_):
        return {"expert": e_, "row": y_, "col": z_}

    def remote(src, dst, send, recv, where):
        return pltpu.make_async_remote_copy(
            src_ref=src, dst_ref=dst, send_sem=send, recv_sem=recv,
            device_id=where, device_id_type=pl.DeviceIdType.MESH,
        )

    def group_peer(k):
        p = lax.rem(y * Z + z + k, Y * Z)
        return p // Z, lax.rem(p, Z)

    def expert_peer(k):
        p = lax.rem(e * Y + y + k, E * Y)
        return p // Y, lax.rem(p, Y)

    barrier = pltpu.get_barrier_semaphore()
    for k in range(1, Y * Z):
        yk, zk = group_peer(k)
        pl.semaphore_signal(barrier, inc=1, device_id=dev(e, yk, zk), device_id_type=pl.DeviceIdType.MESH)
    for k in range(1, E):
        for yk in range(Y):
            pl.semaphore_signal(
                barrier, inc=1, device_id=dev(lax.rem(e + k, E), yk, z), device_id_type=pl.DeviceIdType.MESH
            )

    own_x = pltpu.make_async_copy(
        x_hbm.at[:, pl.ds(pl.multiple_of(y * rows, TILE), rows)],
        xbuf.at[z, pl.ds(pl.multiple_of(y * tokens, tokens), tokens)], local.at[0])
    own_c = pltpu.make_async_copy(
        c_hbm.at[:, pl.ds(pl.multiple_of(z * cols, TILE), cols)],
        cbuf.at[z, pl.ds(pl.multiple_of(y * tokens, tokens), tokens)], local.at[1])
    weights_in = pltpu.make_async_copy(w_hbm, wbuf, local.at[2])
    own_x.start()
    own_c.start()
    weights_in.start()
    pl.semaphore_wait(barrier, Y * Z - 1 + (E - 1) * Y)

    def x_slot(s, q, h):
        return xbuf.at[s, pl.ds(pl.multiple_of(q * tokens + h * piece, piece), piece)]

    def x_own_src(half, h):
        return x_hbm.at[pl.ds(pl.multiple_of(h * piece, piece), piece),
                        pl.ds(pl.multiple_of(half * rows, TILE), rows)]

    def x_right(s, q, h, src):
        return remote(src, x_slot(s, q, h), sx.at[0, s, q, h], rx.at[s, q, h], dev(e, y, lax.rem(z + 1, Z)))

    def x_left(s, q, h, src):
        return remote(src, x_slot(s, q, h), sx.at[1, s, q, h], rx.at[s, q, h], dev(e, y, lax.rem(z + Z - 1, Z)))

    def x_cross(h):
        return remote(x_own_src(other, h), x_slot(z, y, h), sxy.at[h], rx.at[z, y, h], dev(e, other, z))

    def c_slot(s, q):
        return cbuf.at[s, pl.ds(pl.multiple_of(q * tokens, tokens), tokens)]

    def c_src(t):
        return c_hbm.at[:, pl.ds(pl.multiple_of(t * cols, TILE), cols)]

    def c_spread(k):
        t = lax.rem(z + k, Z)
        return remote(c_src(t), c_slot(z, y), sc.at[t], rc.at[z, y], dev(e, y, t))

    def c_cross(s, src):
        return remote(src, c_slot(s, y), scy.at[s], rc.at[s, y], dev(e, other, z))

    for h in range(CHUNKS):
        x_cross(h).start()
    for k in (2, 1, 3) if Z == 4 else range(1, Z):
        c_spread(k).start()
    c_cross(z, c_src(z)).start()

    def send_both(q, source):
        def step(h, carry):
            src = source(h)

            @pl.when(z < Z - 1)
            def _():
                x_right(z, q, h, src).start()

            @pl.when(z > 0)
            def _():
                x_left(z, q, h, src).start()
            return carry
        return step

    lax.fori_loop(0, CHUNKS, send_both(y, lambda h: x_own_src(y, h)), 0)

    def pass_cross(h, carry):
        slot = x_slot(z, other, h)
        x_right(z, other, h, slot).wait_recv()
        return send_both(other, lambda h: x_slot(z, other, h))(h, carry)

    weights_in.wait()

    def weight_tile(r, acc):
        block = wbuf[pl.ds(pl.multiple_of(r * 64, 64), 64), :].astype(jnp.float32)
        block = block * block
        part = block[0:8]
        for i in range(1, 8):
            part = part + block[8 * i:8 * i + 8]
        return acc + part

    weight_acc = lax.fori_loop(0, rows // 64, weight_tile, jnp.zeros((8, cols), jnp.float32))
    weight_sum = jnp.sum(weight_acc, axis=(0, 1), keepdims=True)

    lax.fori_loop(0, CHUNKS, pass_cross, 0)

    def each_side(d, act):
        @pl.when(z >= d)
        def _():
            act(z - d, True)

        @pl.when(z + d < Z)
        def _():
            act(z + d, False)

    def c_step(s, from_left):
        c_spread_recv = remote(c_slot(s, y), c_slot(s, y), sc.at[s], rc.at[s, y], dev(e, y, s))
        c_spread_recv.wait_recv()
        c_cross(s, c_slot(s, y)).start()

    def x_step(q):
        def act(s, from_left):
            def step(h, carry):
                slot = x_slot(s, q, h)
                x_right(s, q, h, slot).wait_recv()
                if from_left:
                    @pl.when(z < Z - 1)
                    def _():
                        x_right(s, q, h, slot).start()
                else:
                    @pl.when(z > 0)
                    def _():
                        x_left(s, q, h, slot).start()
                return carry
            lax.fori_loop(0, CHUNKS, step, 0)
        return act

    def wait_c_other(s):
        remote(c_slot(s, other), c_slot(s, other), scy.at[s], rc.at[s, other], dev(e, other, z)).wait_recv()

    def tile_ds(r):
        return pl.ds(pl.multiple_of(r * TILE, TILE), TILE)

    def compute(s, first):
        def step(r, carry):
            value = lax.dot_general(
                xbuf[s, :, tile_ds(r)], cbuf[s], (((0,), (0,)), ((), ())),
                preferred_element_type=jnp.float32)
            if first:
                grad[tile_ds(r), :] = value
            else:
                grad[tile_ds(r), :] += value
            return carry
        lax.fori_loop(0, tiles, step, 0)

    def compute_side(s, from_left):
        wait_c_other(s)
        compute(s, False)

    each_side(1, c_step)
    each_side(1, x_step(y))
    for d in range(2, Z):
        each_side(d, c_step)
    each_side(1, x_step(other))
    own_x.wait()
    own_c.wait()
    wait_c_other(z)
    compute(z, True)
    for d in range(1, Z):
        if d > 1:
            each_side(d, x_step(y))
            each_side(d, x_step(other))
        each_side(d, compute_side)

    def out_copy(r):
        return pltpu.make_async_copy(grad.at[tile_ds(r)], g_hbm.at[tile_ds(r)], out_sem.at[r])

    def fold_lanes(values):
        part = values[:, 0:128]
        for i in range(1, cols // 128):
            part = part + values[:, 128 * i:128 * i + 128]
        return jnp.sum(part.T, axis=0, keepdims=True)

    def stat_tile(r, acc):
        out_copy(r).start()
        block = grad[tile_ds(r), :]
        block = block * block
        row_part[pl.ds(r, 1), :] = fold_lanes(block)
        return acc + jnp.sum(block, axis=0, keepdims=True)

    col_part[...] = lax.fori_loop(0, tiles, stat_tile, jnp.zeros((1, cols), jnp.float32))

    def row_copy(k):
        return remote(row_part, row_recv.at[z], row_send_sem.at[k], row_recv_sem.at[z],
                      dev(e, y, lax.rem(z + k, Z)))

    col_copy = remote(col_part, col_recv, col_send_sem, col_recv_sem, dev(e, other, z))
    for k in range(1, Z):
        row_copy(k).start()
    col_copy.start()
    row_total = row_part[...]
    for k in range(1, Z):
        s = lax.rem(z + k, Z)
        remote(row_part, row_recv.at[s], row_send_sem.at[k], row_recv_sem.at[s], dev(e, y, s)).wait_recv()
        row_total = row_total + row_recv[s]

    me = e * Y + y
    half_total = jnp.sum(row_total, axis=(0, 1), keepdims=True)
    sq_recv[me] = jnp.broadcast_to(half_total, (8, 128))

    def sq_copy(k):
        ek, yk = expert_peer(k)
        return remote(sq_recv.at[me], sq_recv.at[me], sq_send_sem.at[k], sq_recv_sem.at[me], dev(ek, yk, z))

    for k in range(1, E * Y):
        sq_copy(k).start()
    col_copy.wait_recv()
    col_total = col_part[...] + col_recv[...]
    for k in range(1, E * Y):
        ek, yk = expert_peer(k)
        s = ek * Y + yk
        remote(sq_recv.at[s], sq_recv.at[s], sq_send_sem.at[k], sq_recv_sem.at[s], dev(ek, yk, z)).wait_recv()
    squared_total = sq_recv[0, 0:1, 0:1]
    for s in range(1, E * Y):
        squared_total = squared_total + sq_recv[s, 0:1, 0:1]
    clip = 1.0 / jnp.maximum(1.0, jnp.sqrt(squared_total / total_entries))
    clip_square = clip * clip
    rows_new = decay_rate * row_state[...] + (1.0 - decay_rate) * (clip_square * (row_total / hidden_width) + eps_square)
    cols_new = decay_rate * col_state[...] + (1.0 - decay_rate) * (clip_square * (col_total / model_width) + eps_square)
    new_rows[...] = rows_new
    new_cols[...] = cols_new
    row_part_inverse = 1.0 / rows_new
    row_factor[...] = row_part_inverse
    col_inverse = 1.0 / cols_new

    def update_tile(r, acc):
        block = grad[tile_ds(r), :]
        return acc + fold_lanes(block * block * col_inverse) * row_factor[pl.ds(r, 1), :]

    update_acc = lax.fori_loop(0, tiles, update_tile, jnp.zeros((1, TILE), jnp.float32))
    update_sum = jnp.sum(update_acc, axis=(0, 1), keepdims=True)
    rows_sum = jnp.sum(rows_new, axis=(0, 1), keepdims=True)

    mine = y * Z + z
    line = lax.broadcasted_iota(jnp.int32, (8, 128), 0)
    fin_recv[mine] = jnp.where(line == 0, update_sum, jnp.where(line == 1, weight_sum, rows_sum))

    def fin_copy(k):
        yk, zk = group_peer(k)
        return remote(fin_recv.at[mine], fin_recv.at[mine], fin_send_sem.at[k], fin_recv_sem.at[mine], dev(e, yk, zk))

    for k in range(1, Y * Z):
        fin_copy(k).start()

    for h in range(CHUNKS):
        x_cross(h).wait_send()
    for k in range(1, Z):
        c_spread(k).wait_send()
        row_copy(k).wait_send()
    col_copy.wait_send()
    for s in range(Z):
        c_cross(s, c_slot(s, y)).wait_send()
    for k in range(1, E * Y):
        sq_copy(k).wait_send()

    def sent(i, carry):
        s = i // (Y * CHUNKS)
        q = lax.rem(i // CHUNKS, Y)
        h = lax.rem(i, CHUNKS)

        @pl.when((s <= z) & (z < Z - 1))
        def _():
            x_right(s, q, h, x_slot(s, q, h)).wait_send()

        @pl.when((s >= z) & (z > 0))
        def _():
            x_left(s, q, h, x_slot(s, q, h)).wait_send()
        return carry

    lax.fori_loop(0, Z * Y * CHUNKS, sent, 0)

    for k in range(1, Y * Z):
        yk, zk = group_peer(k)
        s = yk * Z + zk
        remote(fin_recv.at[s], fin_recv.at[s], fin_send_sem.at[k], fin_recv_sem.at[s], dev(e, yk, zk)).wait_recv()
    total = fin_recv[0]
    for s in range(1, Y * Z):
        total = total + fin_recv[s]
    for k in range(1, Y * Z):
        fin_copy(k).wait_send()
    entries = model_width * hidden_width
    row_average = total[2:3, 0:1] / (Z * model_width)
    update_rms = jnp.sqrt(clip_square * row_average * total[0:1, 0:1] / entries)
    weight_rms = jnp.sqrt(total[1:2, 0:1] / entries)
    scalar = weight_rms / jnp.maximum(1.0, update_rms) * clip * jnp.sqrt(row_average)
    row_factor[...] = scalar * lax.rsqrt(rows_new)
    col_factor[...] = lax.rsqrt(cols_new)
    lax.fori_loop(0, tiles, lambda r, c: (out_copy(r).wait(), c)[1], 0)


def body(weights, inputs, cotangents, row_state, col_state):
    matrices, rows, cols = weights.shape
    tokens, model_width = inputs.shape[1:]
    hidden_width = cotangents.shape[2]
    E, Y, Z = lax.axis_size("expert"), lax.axis_size("row"), lax.axis_size("col")
    assert matrices == 1 and Y == 2
    tiles = rows // TILE
    f32 = jnp.float32
    vmem = pl.BlockSpec(memory_space=pltpu.VMEM)
    hbm = pl.BlockSpec(memory_space=pl.ANY)
    dma = pltpu.SemaphoreType.DMA
    grad, new_rows, new_cols, row_factor, col_factor = pl.pallas_call(
        functools.partial(
            kernel, E, Y, Z, float(matrices * E * model_width * hidden_width), float(model_width), float(hidden_width)
        ),
        out_shape=(
            jax.ShapeDtypeStruct((rows, cols), f32),
            jax.ShapeDtypeStruct((tiles, TILE), f32),
            jax.ShapeDtypeStruct((1, cols), f32),
            jax.ShapeDtypeStruct((tiles, TILE), f32),
            jax.ShapeDtypeStruct((1, cols), f32),
        ),
        in_specs=[hbm, hbm, hbm, vmem, vmem],
        out_specs=(hbm, vmem, vmem, vmem, vmem),
        scratch_shapes=[
            pltpu.VMEM((rows, cols), jnp.bfloat16),
            pltpu.VMEM((Z, Y * tokens, rows), jnp.bfloat16),
            pltpu.VMEM((Z, Y * tokens, cols), jnp.bfloat16),
            pltpu.VMEM((rows, cols), f32),
            pltpu.VMEM((tiles, TILE), f32),
            pltpu.VMEM((1, cols), f32),
            pltpu.VMEM((1, cols), f32),
            pltpu.VMEM((Z, tiles, TILE), f32),
            pltpu.VMEM((E * Y, 8, 128), f32),
            pltpu.VMEM((Y * Z, 8, 128), f32),
            dma((2, Z, Y, CHUNKS)),
            dma((Z, Y, CHUNKS)),
            dma((CHUNKS,)),
            dma((Z,)),
            dma((Z, Y)),
            dma((Z,)),
            dma((3,)),
            dma((tiles,)),
            dma((Z,)),
            dma((Z,)),
            dma,
            dma,
            dma((E * Y,)),
            dma((E * Y,)),
            dma((Y * Z,)),
            dma((Y * Z,)),
        ],
        compiler_params=pltpu.CompilerParams(
            collective_id=0, has_side_effects=True, vmem_limit_bytes=58 * 1024 * 1024
        ),
    )(
        weights.reshape(rows, cols), inputs.reshape(tokens, model_width), cotangents.reshape(tokens, hidden_width),
        row_state.reshape(tiles, TILE), col_state,
    )
    scaled = grad * row_factor.reshape(rows, 1) * col_factor
    return scaled[None], new_rows.reshape(1, rows), new_cols


def solution(mesh):
    in_specs = (
        P("expert", "row", "col"),
        P("expert", ("row", "col"), None),
        P("expert", ("row", "col"), None),
        P("expert", "row"),
        P("expert", "col"),
    )
    out_specs = (P("expert", "row", "col"), P("expert", "row"), P("expert", "col"))
    return jax.shard_map(body, mesh=mesh, in_specs=in_specs, out_specs=out_specs, check_vma=False)
```

time: 392 us -> 145 us (0.37)
  blocking collectives: 152 us -> 0 us
  Pallas kernels: 0 us -> 127 us
  other arithmetic: 101 us -> 14 us
  waiting for transfers between devices: 79.9 us -> 0 us
  local copies, waits for them, and re-layouts: 26.6 us -> 3.03 us
  between operations: 16.8 us -> 0.66 us
  matrix products: 15.2 us -> 0 us
    pallas_call x0 -> x1, Pallas kernels: none -> 127 us  [body(): pl.pallas_call(functools.partial(kernel, E, Y, Z, float(matrices * E * mo...]
    all_gather x2 -> x0, waiting for transfers between devices: 79.9 us -> none  [the longest x1 79.9 us: body(): shard_rows = lax.all_gather(inputs_split, 'col', axis=1, tiled=True)]
    all_to_all x2 -> x0, blocking collectives: 76.9 us -> none  [the longest x1 48.8 us: body(): lax.all_to_all(cotangents, 'col', split_axis=2, concat_axis=1, tiled=True)]
    psum x4 -> x0, blocking collectives: 74.8 us -> none  [the longest x1 38.9 us: body(): squared_total = lax.psum(jnp.sum(squares), ('expert', 'row', 'col'))]
    unnamed x2 -> x1, other arithmetic: 63.5 us -> 1.36 us
    reduce_sum x4 -> x0, other arithmetic: 25.1 us -> none  [the longest x1 8.86 us: body(): update_squares = jnp.sum(update * update, axis=(1, 2))]
    unnamed x17 -> x8, local copies, waits for them, and re-layouts: 22.7 us -> 2.42 us
    dot_general x1 -> x0, matrix products: 15.2 us -> none  [body(): jnp.einsum('mkrti,mrktj->mij', input_blocks, hidden_blocks, preferred_ele...]
  transfers between devices with their start and end apart: 2 -> 0, of which waited for: 1 -> 0; matrix products, arithmetic and copies ran while one was open for 9% -> 0% of each run, Pallas kernels for 0% -> 0%
where the time goes in v1:
time: 145 us; the launch traced here: 144 us
  Pallas kernels  127 us (88%)
  other arithmetic  14 us (10%)
  local copies, waits for them, and re-layouts  3.03 us (2%)
    pallas_call x1, Pallas kernels, body(): pl.pallas_call(functools.partial(kernel, E, Y, Z, float(matrices * E * mo...  127 us
    broadcast_in_dim x1, other arithmetic, body(): return (scaled[None], new_rows.reshape(1, rows), new_cols)  11.9 us

profile of v1, /device:TPU:0, one launch (start us, length us, event | category | flops | bytes accessed | tf_op | source)
XLA Modules:
  0.0 144.4 jit_solution(13366487369110250392)
XLA Ops:
  0.6 0.5 broadcast.4
  1.1 1.4 reduce.4
  2.5 0.6 reshape.26.row_state
  3.1 126.7 %shard_map.76 = (f32[2048,1792]{1,0:T(8,128)}, f32[8,256]{1,0:T(8,128)}, f32[1,1792]{1,0:T(1,128)}, f32[8,256]{1,0:T(8,128)}, f32[1,1792]{1,0:T(1,128)}) custom-call(bf16[2048,1792]{1,0:T(8,128)(2,1)} %bitcast.10, bf16[128,4096]{1,0:T(8,128)(2,1)} %bitcast.12, bf16[128,7168]{1,0:T(8,128)(2,1)} %bitcast.11, f32[8,256]{1,0:T(8,128)} %reshape.26.row_state, ...), custom_call_target="tpu_custom_call" | custom-call | tf_op jit(solution)/shard_map/pallas_call | solution.py:348
  129.8 0.7 copy.8
  130.5 0.7 reduce.1
  131.2 0.0 copy-start
  131.2 0.0 copy-start.1
  131.2 11.9 %multiply_bitcast_fusion = f32[1,2048,1792]{2,1,0:T(8,128)} fusion(f32[2048,1792]{1,0:T(8,128)} %get-tuple-element.8, f32[1792]{0:T(1024)S(1)} %reduce.1, f32[2048]{0:T(1024)S(1)} %bitcast.13), kind=kLoop, calls=%fused_computation | loop fusion | flops 7340032 | bytes 29375488 | tf_op jit(solution)/shard_map/broadcast_in_dim | solution.py:397
  143.2 0.0 copy-done
  143.2 0.6 copy.9
  143.8 0.0 copy-done.1
  143.8 0.6 copy.11
Async XLA Ops:
  131.2 12.0 %copy-start = (f32[8,256]{1,0:T(8,128)S(1)}, f32[8,256]{1,0:T(8,128)}, u32[]{:S(2)}) copy-start(f32[8,256]{1,0:T(8,128)} %get-tuple-element.11) | copy-start | bytes 24580
  131.2 12.6 %copy-start.1 = (f32[1,1792]{1,0:T(1,128)S(1)}, f32[1,1792]{1,0:T(1,128)}, u32[]{:S(2)}) copy-start(f32[1,1792]{1,0:T(1,128)} %get-tuple-element.18) | copy-start | bytes 21508

commit v2 on v1

--- a/solution.py
+++ b/solution.py
@@ -17,9 +17,9 @@
 def kernel(
     E, Y, Z, total_entries, model_width, hidden_width,
     w_hbm, x_hbm, c_hbm, row_state, col_state,
-    g_hbm, new_rows, new_cols, row_factor, col_factor,
-    wbuf, xbuf, cbuf, grad, row_part, col_part, col_recv, row_recv, sq_recv, fin_recv,
-    sx, rx, sxy, sc, rc, scy, local, out_sem,
+    grad, new_rows, new_cols, row_factor, col_factor,
+    wbuf, xbuf, cbuf, state, row_part, col_part, col_recv, row_recv, sq_recv, fin_recv,
+    sx, rx, sxy, sc, rc, scy, local,
     row_send_sem, row_recv_sem, col_send_sem, col_recv_sem, sq_send_sem, sq_recv_sem, fin_send_sem, fin_recv_sem,
 ):
     e, y, z = lax.axis_index("expert"), lax.axis_index("row"), lax.axis_index("col")
@@ -27,7 +27,8 @@
     tokens = x_hbm.shape[0]
     rows, cols = grad.shape
     tiles = rows // TILE
-    piece = tokens // CHUNKS
+    piece = rows // CHUNKS
+    chunk_tiles = tiles // CHUNKS
     decay_rate = 1.0 - STEP ** (-0.8)
 
     def dev(e_, y_, z_):
@@ -70,11 +71,10 @@
     pl.semaphore_wait(barrier, Y * Z - 1 + (E - 1) * Y)
 
     def x_slot(s, q, h):
-        return xbuf.at[s, pl.ds(pl.multiple_of(q * tokens + h * piece, piece), piece)]
+        return xbuf.at[s, pl.ds(pl.multiple_of(q * tokens, tokens), tokens), pl.ds(pl.multiple_of(h * piece, piece), piece)]
 
     def x_own_src(half, h):
-        return x_hbm.at[pl.ds(pl.multiple_of(h * piece, piece), piece),
-                        pl.ds(pl.multiple_of(half * rows, TILE), rows)]
+        return x_hbm.at[:, pl.ds(pl.multiple_of(half * rows + h * piece, piece), piece)]
 
     def x_right(s, q, h, src):
         return remote(src, x_slot(s, q, h), sx.at[0, s, q, h], rx.at[s, q, h], dev(e, y, lax.rem(z + 1, Z)))
@@ -154,22 +154,23 @@
         c_spread_recv.wait_recv()
         c_cross(s, c_slot(s, y)).start()
 
+    def x_pass(s, q, h, from_left):
+        slot = x_slot(s, q, h)
+        x_right(s, q, h, slot).wait_recv()
+
+        @pl.when(from_left & (z < Z - 1))
+        def _():
+            x_right(s, q, h, slot).start()
+
+        @pl.when(jnp.logical_not(from_left) & (z > 0))
+        def _():
+            x_left(s, q, h, slot).start()
+
+    def x_all(s, q, from_left):
+        lax.fori_loop(0, CHUNKS, lambda h, carry: (x_pass(s, q, h, from_left), carry)[1], 0)
+
     def x_step(q):
-        def act(s, from_left):
-            def step(h, carry):
-                slot = x_slot(s, q, h)
-                x_right(s, q, h, slot).wait_recv()
-                if from_left:
-                    @pl.when(z < Z - 1)
-                    def _():
-                        x_right(s, q, h, slot).start()
-                else:
-                    @pl.when(z > 0)
-                    def _():
-                        x_left(s, q, h, slot).start()
-                return carry
-            lax.fori_loop(0, CHUNKS, step, 0)
-        return act
+        return lambda s, from_left: x_all(s, q, z >= s)
 
     def wait_c_other(s):
         remote(c_slot(s, other), c_slot(s, other), scy.at[s], rc.at[s, other], dev(e, other, z)).wait_recv()
@@ -193,23 +194,32 @@
         wait_c_other(s)
         compute(s, False)
 
+    from_left = 2 * z >= Z
+    last = jnp.where(from_left, 0, Z - 1)
+
+    def each_near(d, act):
+        @pl.when((z >= d) & (z - d != last))
+        def _():
+            act(z - d, True)
+
+        @pl.when((z + d < Z) & (z + d != last))
+        def _():
+            act(z + d, False)
+
     each_side(1, c_step)
-    each_side(1, x_step(y))
+    each_near(1, x_step(y))
     for d in range(2, Z):
         each_side(d, c_step)
-    each_side(1, x_step(other))
+    each_near(1, x_step(other))
     own_x.wait()
     own_c.wait()
     wait_c_other(z)
     compute(z, True)
-    for d in range(1, Z):
+    for d in range(1, Z - 1):
         if d > 1:
-            each_side(d, x_step(y))
-            each_side(d, x_step(other))
-        each_side(d, compute_side)
-
-    def out_copy(r):
-        return pltpu.make_async_copy(grad.at[tile_ds(r)], g_hbm.at[tile_ds(r)], out_sem.at[r])
+            each_near(d, x_step(y))
+            each_near(d, x_step(other))
+        each_near(d, compute_side)
 
     def fold_lanes(values):
         part = values[:, 0:128]
@@ -217,14 +227,29 @@
             part = part + values[:, 128 * i:128 * i + 128]
         return jnp.sum(part.T, axis=0, keepdims=True)
 
-    def stat_tile(r, acc):
-        out_copy(r).start()
-        block = grad[tile_ds(r), :]
+    for r in range(tiles):
+        state[r:r + 1, :] = row_state[:, r * TILE:(r + 1) * TILE]
+    x_all(last, y, from_left)
+    wait_c_other(last)
+
+    def last_tile(r, acc):
+        @pl.when(lax.rem(r, chunk_tiles) == 0)
+        def _():
+            x_pass(last, other, r // chunk_tiles, from_left)
+
+        block = grad[tile_ds(r), :] + lax.dot_general(
+            xbuf[last, :, tile_ds(r)], cbuf[last], (((0,), (0,)), ((), ())),
+            preferred_element_type=jnp.float32)
+        grad[tile_ds(r), :] = block
         block = block * block
         row_part[pl.ds(r, 1), :] = fold_lanes(block)
-        return acc + jnp.sum(block, axis=0, keepdims=True)
-
-    col_part[...] = lax.fori_loop(0, tiles, stat_tile, jnp.zeros((1, cols), jnp.float32))
+        part = block[0:8]
+        for i in range(1, TILE // 8):
+            part = part + block[8 * i:8 * i + 8]
+        return acc + part
+
+    col_acc = lax.fori_loop(0, tiles, last_tile, jnp.zeros((8, cols), jnp.float32))
+    col_part[...] = jnp.sum(col_acc, axis=0, keepdims=True)
 
     def row_copy(k):
         return remote(row_part, row_recv.at[z], row_send_sem.at[k], row_recv_sem.at[z],
@@ -261,7 +286,7 @@
         squared_total = squared_total + sq_recv[s, 0:1, 0:1]
     clip = 1.0 / jnp.maximum(1.0, jnp.sqrt(squared_total / total_entries))
     clip_square = clip * clip
-    rows_new = decay_rate * row_state[...] + (1.0 - decay_rate) * (clip_square * (row_total / hidden_width) + eps_square)
+    rows_new = decay_rate * state[...] + (1.0 - decay_rate) * (clip_square * (row_total / hidden_width) + eps_square)
     cols_new = decay_rate * col_state[...] + (1.0 - decay_rate) * (clip_square * (col_total / model_width) + eps_square)
     new_rows[...] = rows_new
     new_cols[...] = cols_new
@@ -331,7 +356,30 @@
     scalar = weight_rms / jnp.maximum(1.0, update_rms) * clip * jnp.sqrt(row_average)
     row_factor[...] = scalar * lax.rsqrt(rows_new)
     col_factor[...] = lax.rsqrt(cols_new)
-    lax.fori_loop(0, tiles, lambda r, c: (out_copy(r).wait(), c)[1], 0)
+
+
+def scale_kernel(grad, rows_in, cols_in, row_factor, col_factor, out, rows_out, cols_out, held, sems):
+    rows, cols = grad.shape
+    tiles = rows // TILE
+
+    def copy(r):
+        span = pl.ds(pl.multiple_of(r * TILE, TILE), TILE)
+        return pltpu.make_async_copy(held.at[span], out.at[span], sems.at[r])
+
+    def tile(r, carry):
+        span = pl.ds(pl.multiple_of(r * TILE, TILE), TILE)
+        factor = jnp.broadcast_to(row_factor[pl.ds(r, 1), :], (128, TILE)).T
+        for i in range(cols // 128):
+            lanes = slice(128 * i, 128 * i + 128)
+            held[span, lanes] = grad[span, lanes] * factor * col_factor[:, lanes]
+        copy(r).start()
+        return carry
+
+    lax.fori_loop(0, tiles, tile, 0)
+    for r in range(tiles):
+        rows_out[:, r * TILE:(r + 1) * TILE] = rows_in[r:r + 1, :]
+    cols_out[...] = cols_in[...]
+    lax.fori_loop(0, tiles, lambda r, c: (copy(r).wait(), c)[1], 0)
 
 
 def body(weights, inputs, cotangents, row_state, col_state):
@@ -350,19 +398,19 @@
             kernel, E, Y, Z, float(matrices * E * model_width * hidden_width), float(model_width), float(hidden_width)
         ),
         out_shape=(
-            jax.ShapeDtypeStruct((rows, cols), f32),
-            jax.ShapeDtypeStruct((tiles, TILE), f32),
-            jax.ShapeDtypeStruct((1, cols), f32),
-            jax.ShapeDtypeStruct((tiles, TILE), f32),
-            jax.ShapeDtypeStruct((1, cols), f32),
+            pltpu.VMEM((rows, cols), f32),
+            pltpu.VMEM((tiles, TILE), f32),
+            pltpu.VMEM((1, cols), f32),
+            pltpu.VMEM((tiles, TILE), f32),
+            pltpu.VMEM((1, cols), f32),
         ),
         in_specs=[hbm, hbm, hbm, vmem, vmem],
-        out_specs=(hbm, vmem, vmem, vmem, vmem),
+        out_specs=(vmem, vmem, vmem, vmem, vmem),
         scratch_shapes=[
             pltpu.VMEM((rows, cols), jnp.bfloat16),
             pltpu.VMEM((Z, Y * tokens, rows), jnp.bfloat16),
             pltpu.VMEM((Z, Y * tokens, cols), jnp.bfloat16),
-            pltpu.VMEM((rows, cols), f32),
+            pltpu.VMEM((tiles, TILE), f32),
             pltpu.VMEM((tiles, TILE), f32),
             pltpu.VMEM((1, cols), f32),
             pltpu.VMEM((1, cols), f32),
@@ -376,7 +424,6 @@
             dma((Z, Y)),
             dma((Z,)),
             dma((3,)),
-            dma((tiles,)),
             dma((Z,)),
             dma((Z,)),
             dma,
@@ -387,14 +434,25 @@
             dma((Y * Z,)),
         ],
         compiler_params=pltpu.CompilerParams(
-            collective_id=0, has_side_effects=True, vmem_limit_bytes=58 * 1024 * 1024
+            collective_id=0, has_side_effects=True, vmem_limit_bytes=44 * 1024 * 1024
         ),
     )(
         weights.reshape(rows, cols), inputs.reshape(tokens, model_width), cotangents.reshape(tokens, hidden_width),
-        row_state.reshape(tiles, TILE), col_state,
+        row_state, col_state,
     )
-    scaled = grad * row_factor.reshape(rows, 1) * col_factor
-    return scaled[None], new_rows.reshape(1, rows), new_cols
+    scaled, new_rows, new_cols = pl.pallas_call(
+        scale_kernel,
+        out_shape=(
+            jax.ShapeDtypeStruct((rows, cols), f32),
+            jax.ShapeDtypeStruct((1, rows), f32),
+            jax.ShapeDtypeStruct((1, cols), f32),
+        ),
+        in_specs=[vmem] * 5,
+        out_specs=(hbm, vmem, vmem),
+        scratch_shapes=[pltpu.VMEM((rows, cols), f32), dma((tiles,))],
+        compiler_params=pltpu.CompilerParams(vmem_limit_bytes=17 * 1024 * 1024),
+    )(grad, new_rows, new_cols, row_factor, col_factor)
+    return scaled[None], new_rows, new_cols
 
 
 def solution(mesh):

time: 145 us -> 128 us (0.88)
  other arithmetic: 14 us -> 0 us
  local copies, waits for them, and re-layouts: 3.03 us -> 0 us
    broadcast_in_dim x1 -> x0, other arithmetic: 11.9 us -> none  [body(): return (scaled[None], new_rows.reshape(1, rows), new_cols)]
    pallas_call x0 -> x1, Pallas kernels: none -> 6.14 us  [body(): pl.pallas_call(scale_kernel, out_shape=(jax.ShapeDtypeStruct((rows, cols)...]
    pallas_call x1, Pallas kernels: 127 us -> 121 us  [body(): pl.pallas_call(functools.partial(kernel, E, Y, Z, float(matrices * E * mo...]
    unnamed x8 -> x0, local copies, waits for them, and re-layouts: 2.42 us -> none
where the time goes in v2:
time: 128 us
  Pallas kernels  128 us (100%)
    pallas_call x1, Pallas kernels, body(): pl.pallas_call(functools.partial(kernel, E, Y, Z, float(matrices * E * mo...  121 us
    pallas_call x1, Pallas kernels, body(): pl.pallas_call(scale_kernel, out_shape=(jax.ShapeDtypeStruct((rows, cols)...  6.14 us

profile of v2, /device:TPU:0, one launch (start us, length us, event | category | flops | bytes accessed | tf_op | source)
XLA Modules:
  0.0 128.2 jit_solution(5763131460034138419)
XLA Ops:
  0.6 121.4 %shard_map.76 = (f32[2048,1792]{1,0:T(8,128)S(1)}, f32[8,256]{1,0:T(8,128)S(1)}, f32[1,1792]{1,0:T(1,128)S(1)}, f32[8,256]{1,0:T(8,128)S(1)}, f32[1,1792]{1,0:T(1,128)S(1)}) custom-call(bf16[2048,1792]{1,0:T(8,128)(2,1)} %bitcast.4, bf16[128,4096]{1,0:T(8,128)(2,1)} %bitcast.6, bf16[128,7168]{1,0:T(8,128)(2,1)} %bitcast.5, f32[1,2048]{1,0:T(1,128)} %row_state.1, ...), custom_call_target="tpu_custom_call" | custom-call | tf_op jit(solution)/shard_map/pallas_call | solution.py:396
  122.1 6.1 %shard_map.77 = (f32[2048,1792]{1,0:T(8,128)}, f32[1,2048]{1,0:T(1,128)}, f32[1,1792]{1,0:T(1,128)}) custom-call(f32[2048,1792]{1,0:T(8,128)S(1)} %get-tuple-element.11.grad, f32[8,256]{1,0:T(8,128)S(1)} %get-tuple-element.12.rows_in, f32[1,1792]{1,0:T(1,128)S(1)} %get-tuple-element.13.cols_in, f32[8,256]{1,0:T(8,128)S(1)} %get-tuple-element.14.row_factor, ...), custom_call_target="tpu_custom_call" | custom-call | tf_op jit(solution)/shard_map/pallas_call | solution.py:443

commit v3 on v2

--- a/solution.py
+++ b/solution.py
@@ -44,19 +44,20 @@
         p = lax.rem(y * Z + z + k, Y * Z)
         return p // Z, lax.rem(p, Z)
 
-    def expert_peer(k):
-        p = lax.rem(e * Y + y + k, E * Y)
-        return p // Y, lax.rem(p, Y)
+    everyone = E * Y * Z
+    me = (e * Y + y) * Z + z
+
+    def any_peer(k):
+        p = lax.rem(me + k, everyone)
+        return p, dev(p // (Y * Z), lax.rem(p // Z, Y), lax.rem(p, Z))
 
     barrier = pltpu.get_barrier_semaphore()
-    for k in range(1, Y * Z):
-        yk, zk = group_peer(k)
-        pl.semaphore_signal(barrier, inc=1, device_id=dev(e, yk, zk), device_id_type=pl.DeviceIdType.MESH)
-    for k in range(1, E):
-        for yk in range(Y):
-            pl.semaphore_signal(
-                barrier, inc=1, device_id=dev(lax.rem(e + k, E), yk, z), device_id_type=pl.DeviceIdType.MESH
-            )
+
+    def greet(k, carry):
+        pl.semaphore_signal(barrier, inc=1, device_id=any_peer(k)[1], device_id_type=pl.DeviceIdType.MESH)
+        return carry
+
+    lax.fori_loop(1, everyone, greet, 0)
 
     own_x = pltpu.make_async_copy(
         x_hbm.at[:, pl.ds(pl.multiple_of(y * rows, TILE), rows)],
@@ -68,7 +69,7 @@
     own_x.start()
     own_c.start()
     weights_in.start()
-    pl.semaphore_wait(barrier, Y * Z - 1 + (E - 1) * Y)
+    pl.semaphore_wait(barrier, everyone - 1)
 
     def x_slot(s, q, h):
         return xbuf.at[s, pl.ds(pl.multiple_of(q * tokens, tokens), tokens), pl.ds(pl.multiple_of(h * piece, piece), piece)]
@@ -256,34 +257,32 @@
                       dev(e, y, lax.rem(z + k, Z)))
 
     col_copy = remote(col_part, col_recv, col_send_sem, col_recv_sem, dev(e, other, z))
+    own_total = jnp.sum(row_part[...], axis=(0, 1), keepdims=True)
+    sq_recv[me] = jnp.broadcast_to(own_total, (1, 128))
+
+    def sq_copy(k):
+        return remote(sq_recv.at[me], sq_recv.at[me], sq_send_sem.at[k], sq_recv_sem.at[me], any_peer(k)[1])
+
     for k in range(1, Z):
         row_copy(k).start()
     col_copy.start()
+    lax.fori_loop(1, everyone, lambda k, carry: (sq_copy(k).start(), carry)[1], 0)
     row_total = row_part[...]
     for k in range(1, Z):
         s = lax.rem(z + k, Z)
         remote(row_part, row_recv.at[s], row_send_sem.at[k], row_recv_sem.at[s], dev(e, y, s)).wait_recv()
         row_total = row_total + row_recv[s]
 
-    me = e * Y + y
-    half_total = jnp.sum(row_total, axis=(0, 1), keepdims=True)
-    sq_recv[me] = jnp.broadcast_to(half_total, (8, 128))
-
-    def sq_copy(k):
-        ek, yk = expert_peer(k)
-        return remote(sq_recv.at[me], sq_recv.at[me], sq_send_sem.at[k], sq_recv_sem.at[me], dev(ek, yk, z))
-
-    for k in range(1, E * Y):
-        sq_copy(k).start()
     col_copy.wait_recv()
     col_total = col_part[...] + col_recv[...]
-    for k in range(1, E * Y):
-        ek, yk = expert_peer(k)
-        s = ek * Y + yk
-        remote(sq_recv.at[s], sq_recv.at[s], sq_send_sem.at[k], sq_recv_sem.at[s], dev(ek, yk, z)).wait_recv()
-    squared_total = sq_recv[0, 0:1, 0:1]
-    for s in range(1, E * Y):
-        squared_total = squared_total + sq_recv[s, 0:1, 0:1]
+
+    def sq_arrived(k, carry):
+        p, where = any_peer(k)
+        remote(sq_recv.at[p], sq_recv.at[p], sq_send_sem.at[k], sq_recv_sem.at[p], where).wait_recv()
+        return carry
+
+    lax.fori_loop(1, everyone, sq_arrived, 0)
+    squared_total = jnp.sum(sq_recv[...], axis=0)[:, 0:1]
     clip = 1.0 / jnp.maximum(1.0, jnp.sqrt(squared_total / total_entries))
     clip_square = clip * clip
     rows_new = decay_rate * state[...] + (1.0 - decay_rate) * (clip_square * (row_total / hidden_width) + eps_square)
@@ -321,8 +320,7 @@
     col_copy.wait_send()
     for s in range(Z):
         c_cross(s, c_slot(s, y)).wait_send()
-    for k in range(1, E * Y):
-        sq_copy(k).wait_send()
+    lax.fori_loop(1, everyone, lambda k, carry: (sq_copy(k).wait_send(), carry)[1], 0)
 
     def sent(i, carry):
         s = i // (Y * CHUNKS)
@@ -415,7 +413,7 @@
             pltpu.VMEM((1, cols), f32),
             pltpu.VMEM((1, cols), f32),
             pltpu.VMEM((Z, tiles, TILE), f32),
-            pltpu.VMEM((E * Y, 8, 128), f32),
+            pltpu.VMEM((E * Y * Z, 1, 128), f32),
             pltpu.VMEM((Y * Z, 8, 128), f32),
             dma((2, Z, Y, CHUNKS)),
             dma((Z, Y, CHUNKS)),
@@ -428,8 +426,8 @@
             dma((Z,)),
             dma,
             dma,
-            dma((E * Y,)),
-            dma((E * Y,)),
+            dma((E * Y * Z,)),
+            dma((E * Y * Z,)),
             dma((Y * Z,)),
             dma((Y * Z,)),
         ],

time: 128 us -> 128 us (level)
  no operation moved by 1% of the time
where the time goes in v3:
time: 128 us
  Pallas kernels  127 us (99%)
    pallas_call x1, Pallas kernels, body(): pl.pallas_call(functools.partial(kernel, E, Y, Z, float(matrices * E * mo...  121 us
    pallas_call x1, Pallas kernels, body(): pl.pallas_call(scale_kernel, out_shape=(jax.ShapeDtypeStruct((rows, cols)...  6.14 us

profile of v3, /device:TPU:0, one launch (start us, length us, event | category | flops | bytes accessed | tf_op | source)
XLA Modules:
  0.0 127.7 jit_solution(17058831293496866874)
XLA Ops:
  0.6 121.0 %shard_map.76 = (f32[2048,1792]{1,0:T(8,128)S(1)}, f32[8,256]{1,0:T(8,128)S(1)}, f32[1,1792]{1,0:T(1,128)S(1)}, f32[8,256]{1,0:T(8,128)S(1)}, f32[1,1792]{1,0:T(1,128)S(1)}) custom-call(bf16[2048,1792]{1,0:T(8,128)(2,1)} %bitcast.4, bf16[128,4096]{1,0:T(8,128)(2,1)} %bitcast.6, bf16[128,7168]{1,0:T(8,128)(2,1)} %bitcast.5, f32[1,2048]{1,0:T(1,128)} %row_state.1, ...), custom_call_target="tpu_custom_call" | custom-call | tf_op jit(solution)/shard_map/pallas_call | solution.py:394
  121.6 6.1 %shard_map.77 = (f32[2048,1792]{1,0:T(8,128)}, f32[1,2048]{1,0:T(1,128)}, f32[1,1792]{1,0:T(1,128)}) custom-call(f32[2048,1792]{1,0:T(8,128)S(1)} %get-tuple-element.11.grad, f32[8,256]{1,0:T(8,128)S(1)} %get-tuple-element.12.rows_in, f32[1,1792]{1,0:T(1,128)S(1)} %get-tuple-element.13.cols_in, f32[8,256]{1,0:T(8,128)S(1)} %get-tuple-element.14.row_factor, ...), custom_call_target="tpu_custom_call" | custom-call | tf_op jit(solution)/shard_map/pallas_call | solution.py:441
